TPU v7x, 32 devices: a whole 2x2x4 slice. The times are simulated.
32 devices in a mesh: gx: 2 (over core), gy: 4 (over y, x), gz: 4 (over z).
Axes of the slice: x: 2, y: 2, z: 4, core: 2. Of those that a mesh axis runs over, the one named last changes fastest.
Arguments:
- raw_weight: float32 [128, 27, 128], P(('gx', 'gy')), may hold values from -6 to 6
- inputs: bfloat16 [16, 64, 64, 128], P('gx', 'gy', 'gz'), may hold values from -6 to 6
- cotangent: bfloat16 [16, 64, 64, 128], P('gx', 'gy', 'gz'), may hold values from -0.099609375 to 0.099609375
Outputs:
- input_grad: bfloat16 [16, 64, 64, 128], P('gx', 'gy', 'gz')
- weight_grad: float32 [128, 27, 128], P(('gx', 'gy'))
All inputs are finite; a program needn't handle non-finite values.
Results may differ from a plain program's by a relative error of at most 0.0049.
Values may be sent and summed in bfloat16 or wider, within the bound.
A program may use at most 64 MiB of HBM per device.

v0:
```python
import jax
import jax.numpy as jnp
from jax import lax
from jax.sharding import PartitionSpec as P

var_eps = 1e-05
norm_eps = 1e-06
clip_norm = 600.0


def with_halo(cells, sides, width):
    for axis, dim in sides:
        count = lax.axis_size(axis)
        ends = count - 1
        head = lax.slice_in_dim(cells, 0, width, axis=dim)
        tail = lax.slice_in_dim(cells, cells.shape[dim] - width, cells.shape[dim], axis=dim)
        cells = jnp.concatenate(
            [
                lax.ppermute(tail, axis, [(i, (i + 1) % count) for i in range(ends)]),
                cells,
                lax.ppermute(head, axis, [((i + 1) % count, i) for i in range(ends)]),
            ],
            axis=dim,
        )
    return cells


def tap_view(padded, tap_a, tap_b, tap_c, extent):
    view = padded[
        2 - tap_a : 2 - tap_a + extent[0],
        2 - tap_b : 2 - tap_b + extent[1],
        2 - tap_c : 2 - tap_c + extent[2],
        :,
    ]
    return view.reshape(-1, view.shape[-1])


def input_rows(padded, extent, block_rows):
    row_count = block_rows.shape[0]
    total = jnp.zeros((extent[0] * extent[1] * extent[2], row_count), jnp.float32)
    for tap_a in range(3):
        for tap_b in range(3):
            for tap_c in range(3):
                tap_index = tap_a * 9 + tap_b * 3 + tap_c
                view = tap_view(padded, tap_a, tap_b, tap_c, extent)
                total = total + lax.dot_general(
                    view,
                    block_rows[:, tap_index, :],
                    (((1,), (1,)), ((), ())),
                    preferred_element_type=jnp.float32,
                )
    return total.astype(jnp.bfloat16).reshape(extent[0], extent[1], extent[2], row_count)


def filter_terms(padded, flat_in, extent):
    pieces = []
    for tap_a in range(3):
        for tap_b in range(3):
            for tap_c in range(3):
                view = tap_view(padded, tap_a, tap_b, tap_c, extent)
                pieces.append(
                    lax.dot_general(
                        flat_in, view, (((0,), (0,)), ((), ())), preferred_element_type=jnp.float32
                    )
                )
    return jnp.stack(pieces, axis=1)


def on_device(raw_weight, inputs, cotangent):
    extent = inputs.shape[:3]
    channels = inputs.shape[3]
    fan_count = channels * raw_weight.shape[1]
    padded = with_halo(cotangent, (("gx", 0), ("gy", 1), ("gz", 2)), 1)
    flat_in = inputs.reshape(-1, channels)
    sum_first, sum_second = lax.psum(
        (jnp.sum(raw_weight, axis=(0, 1)), jnp.sum(raw_weight * raw_weight, axis=(0, 1))),
        ("gx", "gy"),
    )
    mean_out = sum_first / fan_count
    var_out = sum_second / fan_count - mean_out * mean_out
    inv_std = lax.rsqrt(var_out + var_eps)
    std_float = (raw_weight - mean_out) * inv_std
    std_whole = lax.all_gather(std_float.astype(jnp.bfloat16), ("gx", "gy"), axis=0, tiled=True)
    input_grad = input_rows(padded, extent, std_whole)
    local_terms = filter_terms(padded, flat_in, extent)
    column_sum = lax.psum(local_terms, "gz")
    filter_grad = lax.psum_scatter(column_sum, ("gx", "gy"), scatter_dimension=0, tiled=True)
    local_grad = jnp.sum(filter_grad, axis=(0, 1))
    local_cross = jnp.sum(filter_grad * std_float, axis=(0, 1))
    local_square = jnp.sum(filter_grad * filter_grad, axis=(0, 1))
    sum_grad, sum_cross, sum_square = lax.psum(
        (local_grad, local_cross, local_square), ("gx", "gy")
    )
    mean_grad = sum_grad / fan_count
    mean_cross = sum_cross / fan_count
    raw_grad = inv_std * (filter_grad - mean_grad - std_float * mean_cross)
    per_output = sum_square - 2.0 * mean_grad * sum_grad - 2.0 * mean_cross * sum_cross
    per_output = (
        per_output
        + fan_count * mean_grad * mean_grad
        + fan_count * mean_cross * mean_cross * var_out / (var_out + var_eps)
    )
    square_sum = jnp.sum(inv_std * inv_std * per_output)
    scale = jnp.minimum(1.0, clip_norm * lax.rsqrt(square_sum + norm_eps))
    return (input_grad, raw_grad * scale)


def solution(mesh):
    in_specs = (P(("gx", "gy"), None, None), P("gx", "gy", "gz", None), P("gx", "gy", "gz", None))
    out_specs = (P("gx", "gy", "gz", None), P(("gx", "gy"), None, None))
    return jax.shard_map(
        on_device, mesh=mesh, in_specs=in_specs, out_specs=out_specs, check_vma=False
    )
```

profile of v0, /device:TPU:0, one launch (start us, length us, event | category | flops | bytes accessed | tf_op | source)
XLA Modules:
  0.0 215.6 jit_solution(4366381669883090917)
XLA Ops:
  7.2 0.9 fusion.68
  8.2 2.4 %collective-permute-start = (bf16[1,16,16,128]{3,2,1,0:T(8,128)(2,1)S(1)}, bf16[1,16,16,128]{3,2,1,0:T(8,128)(2,1)S(1)}, u32[]{:S(2)}, u32[]{:S(2)}) collective-permute-start(bf16[1,16,16,128]{3,2,1,0:T(8,128)(2,1)S(1)} %get-tuple-element.51), channel_id=1, source_target_pairs={{0,16},{1,17},{2,18},{3,19},{4,20},{5,21},{6,22},{7,23},{8,24},{9,... | collective-permute-start | bytes 196616 | tf_op jit(solution)/shard_map/ppermute | solution.py:19
  10.6 1.3 collective-permute-start.1
  11.9 1.4 constant_dynamic-update-slice_fusion.5
  13.8 1.3 collective-permute-start.3
  15.1 4.8 %collective-permute-start.2 = (bf16[10,1,16,128]{3,2,1,0:T(8,128)(2,1)S(1)}, bf16[10,1,16,128]{3,2,1,0:T(8,128)(2,1)S(1)}, u32[]{:S(2)}, u32[]{:S(2)}) collective-permute-start(bf16[10,1,16,128]{3,2,1,0:T(8,128)(2,1)S(1)} %get-tuple-element.45), channel_id=1, source_target_pairs={{0,4},{4,8},{8,12},{1,5},{5,9},{9,13},{2,6},{6,10},{10,14},{3,7},{... | collective-permute-start | bytes 122888 | tf_op jit(solution)/shard_map/ppermute | solution.py:19
  20.3 1.3 collective-permute-done.2
  21.8 1.3 collective-permute-start.4
  23.1 4.6 %collective-permute-start.5 = (bf16[10,18,1,128]{3,2,1,0:T(2,128)(2,1)S(1)}, bf16[10,18,1,128]{3,2,1,0:T(2,128)(2,1)S(1)}, u32[]{:S(2)}, u32[]{:S(2)}) collective-permute-start(bf16[10,18,1,128]{3,2,1,0:T(2,128)(2,1)S(1)} %get-tuple-element.35), channel_id=1, source_target_pairs={{0,1},{1,2},{2,3},{4,5},{5,6},{6,7},{8,9},{9,10},{10,11},{12,13},{... | collective-permute-start | bytes 138248 | tf_op jit(solution)/shard_map/ppermute | solution.py:19
  28.3 1.5 collective-permute-done.5
  29.8 0.8 pad_maximum_fusion.2
  30.6 1.0 fusion.29
  31.6 1.0 fusion.10
  32.6 1.0 fusion.28
  33.5 1.0 fusion.27
  34.5 1.0 fusion.9
  35.5 1.0 fusion.26
  36.5 1.0 fusion.25
  37.4 1.0 fusion.8
  38.4 1.0 fusion.24
  39.4 1.0 fusion.23
  40.4 1.0 fusion.7
  41.3 1.0 fusion.22
  42.3 1.0 fusion.21
  43.3 1.0 fusion.20
  44.3 1.0 fusion.19
  45.3 1.0 fusion.18
  46.3 1.0 fusion.6
  47.2 1.0 fusion.17
  48.2 1.0 fusion.16
  49.2 1.0 fusion.5
  50.1 1.0 fusion.15
  51.1 1.0 fusion.14
  52.1 1.0 fusion.4
  53.1 1.0 fusion.13
  54.1 1.0 fusion.12
  55.0 1.0 fusion.3
  56.0 1.0 fusion.11
  57.0 3.1 %copy.12 = f32[128,27,128]{2,1,0:T(8,128)} copy(f32[128,27,128]{0,2,1:T(8,128)} %fusion.11) | data formatting | bytes 3538944 | tf_op jit(solution)/shard_map/stack | solution.py:66
  60.2 1.0 multiply_reduce_fusion.2
  61.2 16.7 %all-reduce.1 = (f32[128]{0:T(128)S(1)}, f32[128]{0:T(128)S(1)}) all-reduce(f32[128]{0:T(128)S(1)} %get-tuple-element.8, f32[128]{0:T(128)S(1)} %get-tuple-element.7), channel_id=1, replica_groups=mesh['gx'=2,'gy'=4,'gz'=4] {'gx','gy'}, use_global_device_ids=true, to_apply=%region_1.0 | all-reduce | flops 256 | bytes 2048 | tf_op jit(solution)/shard_map/psum | solution.py:75
  77.9 1.9 slice.299
  79.8 1.9 slice.338
  81.7 1.7 fusion.32
  83.4 22.2 %reduce-scatter.2.cloned.1.call-done = f32[16,27,128]{2,1,0:T(8,128)} async-done(((f32[128,27,128]{2,1,0:T(8,128)}), f32[16,27,128]{2,1,0:T(8,128)}) %reduce-scatter.2.cloned.1.call-update) | async-done | bytes 221200 | tf_op jit(solution)/shard_map/reduce_scatter | solution.py:87
  105.6 1.8 copy.13
  107.4 3.7 %fusion.65 = (bf16[8,16,16,128]{3,2,1,0:T(8,128)(2,1)}, bf16[8,16,16,128]{3,2,1,0:T(8,128)(2,1)}, bf16[8,16,16,128]{3,2,1,0:T(8,128)(2,1)}, bf16[8,16,16,128]{3,...) fusion(bf16[10,18,17,128]{3,2,1,0:T(8,128)(2,1)S(1)} %get-tuple, ...), kind=kLoop, calls=%fused_computation.177 | loop fusion | bytes 18874368 | tf_op jit(solution)/shard_map/slice | solution.py:29
  111.1 32.5 %all-reduce.4.cloned.1.call-done = f32[16,27,128]{2,0,1:T(8,128)} async-done(((f32[16,27,128]{2,0,1:T(8,128)}), f32[16,27,128]{2,0,1:T(8,128)}) %all-reduce.4.cloned.1.call-update) | async-done | bytes 221200 | tf_op jit(solution)/shard_map/psum | solution.py:86
  143.6 1.1 multiply_reduce_fusion
  144.8 14.4 %all-reduce = (f32[128]{0:T(128)S(1)}, f32[128]{0:T(128)S(1)}, f32[128]{0:T(128)S(1)}) all-reduce(f32[128]{0:T(128)S(1)} %get-tuple-element.5, f32[128]{0:T(128)S(1)} %get-tuple-element.6, f32[128]{0:T(128)S(1)} %get-tuple-element.4), channel_id=1, replica_groups=mesh['gx'=2,'gy'=4,'gz'=4] {'gx','gy'}, use_global_device_ids=true, to_apply=%region_9.0 | all-reduce | flops 384 | bytes 3072 | tf_op jit(solution)/shard_map/psum | solution.py:91
  160.5 1.8 multiply_multiply_fusion
  162.3 27.9 %all_gather.3 = bf16[128,27,128]{2,0,1:T(8,128)(2,1)S(1)} all-gather(bf16[16,27,128]{2,0,1:T(8,128)(2,1)S(1)} %get-tuple-element.53), channel_id=1, replica_groups=mesh['gx'=2,'gy'=4,'gz'=4] {'gx','gy'}, dimensions={0}, use_global_device_ids=true | all-gather | bytes 995328 | tf_op jit(solution)/shard_map/all_gather | solution.py:83
  191.8 0.7 copy-done.18
  193.2 0.7 copy-done.17
  194.6 0.7 copy-done.16
  196.0 0.7 copy-done.26
  197.4 0.7 copy-done.13
  198.8 0.6 copy-done.12
  200.1 0.6 copy-done.25
  201.5 0.6 copy-done.9
  202.9 0.6 copy-done.8
  204.3 0.6 copy-done.21
  207.0 0.6 copy-done.4
  207.7 1.1 fusion.2
  (89 shorter events, 12.4 us)
Async XLA Ops:
  7.2 23.5 %copy-start = (bf16[8,16,16,128]{3,2,1,0:T(8,128)(2,1)S(1)}, bf16[8,16,16,128]{3,2,1,0:T(8,128)(2,1)}, u32[]{:S(2)}) copy-start(bf16[8,16,16,128]{3,2,1,0:T(8,128)(2,1)} %param.4) | copy-start | bytes 1572868
  7.2 98.4 %reduce-scatter.2.cloned.1.call-start = ((), (), s32[]{:S(2)}) async-start(), calls=%async_computation.1 | async-start | bytes 2359296 | tf_op jit(solution)/shard_map/reduce_scatter | solution.py:87
  8.2 3.7 %collective-permute-start = (bf16[1,16,16,128]{3,2,1,0:T(8,128)(2,1)S(1)}, bf16[1,16,16,128]{3,2,1,0:T(8,128)(2,1)S(1)}, u32[]{:S(2)}, u32[]{:S(2)}) collective-permute-start(bf16[1,16,16,128]{3,2,1,0:T(8,128)(2,1)S(1)} %get-tuple-element.51), channel_id=1, source_target_pairs={{0,16},{1,17},{2,18},{3,19},{4,20},{5,21},{6,22},{7,23},{8,24},{9,... | collective-permute-start | bytes 196616 | tf_op jit(solution)/shard_map/ppermute | solution.py:19
  10.6 3.1 %collective-permute-start.1 = (bf16[1,16,16,128]{3,2,1,0:T(8,128)(2,1)S(1)}, bf16[1,16,16,128]{3,2,1,0:T(8,128)(2,1)S(1)}, u32[]{:S(2)}, u32[]{:S(2)}) collective-permute-start(bf16[1,16,16,128]{3,2,1,0:T(8,128)(2,1)S(1)} %get-tuple-element.50), channel_id=1, source_target_pairs={{16,0},{17,1},{18,2},{19,3},{20,4},{21,5},{22,6},{23,7},{24,8},{25... | collective-permute-start | bytes 196616 | tf_op jit(solution)/shard_map/ppermute | solution.py:21
  13.3 38.8 %copy-start.29 = (bf16[9,16,16,128]{3,2,1,0:T(8,128)(2,1)}, bf16[9,16,16,128]{3,2,1,0:T(8,128)(2,1)S(1)}, u32[]{:S(2)}) copy-start(bf16[9,16,16,128]{3,2,1,0:T(8,128)(2,1)S(1)} %get-tuple-element.47) | copy-start | bytes 1769476
  13.7 20.8 %copy-start.28 = (bf16[9,16,16,128]{3,2,1,0:T(8,128)(2,1)}, bf16[9,16,16,128]{3,2,1,0:T(8,128)(2,1)S(1)}, u32[]{:S(2)}) copy-start(bf16[9,16,16,128]{3,2,1,0:T(8,128)(2,1)S(1)} %get-tuple-element.56) | copy-start | bytes 1769476
  13.8 6.6 %collective-permute-start.3 = (bf16[10,1,16,128]{3,2,1,0:T(8,128)(2,1)S(1)}, bf16[10,1,16,128]{3,2,1,0:T(8,128)(2,1)S(1)}, u32[]{:S(2)}, u32[]{:S(2)}) collective-permute-start(bf16[10,1,16,128]{3,2,1,0:T(8,128)(2,1)S(1)} %get-tuple-element.46), channel_id=1, source_target_pairs={{4,0},{8,4},{12,8},{5,1},{9,5},{13,9},{6,2},{10,6},{14,10},{7,3},{... | collective-permute-start | bytes 122888 | tf_op jit(solution)/shard_map/ppermute | solution.py:21
  15.1 6.6 %collective-permute-start.2 = (bf16[10,1,16,128]{3,2,1,0:T(8,128)(2,1)S(1)}, bf16[10,1,16,128]{3,2,1,0:T(8,128)(2,1)S(1)}, u32[]{:S(2)}, u32[]{:S(2)}) collective-permute-start(bf16[10,1,16,128]{3,2,1,0:T(8,128)(2,1)S(1)} %get-tuple-element.45), channel_id=1, source_target_pairs={{0,4},{4,8},{8,12},{1,5},{5,9},{9,13},{2,6},{6,10},{10,14},{3,7},{... | collective-permute-start | bytes 122888 | tf_op jit(solution)/shard_map/ppermute | solution.py:19
  21.8 6.5 %collective-permute-start.4 = (bf16[10,18,1,128]{3,2,1,0:T(2,128)(2,1)S(1)}, bf16[10,18,1,128]{3,2,1,0:T(2,128)(2,1)S(1)}, u32[]{:S(2)}, u32[]{:S(2)}) collective-permute-start(bf16[10,18,1,128]{3,2,1,0:T(2,128)(2,1)S(1)} %get-tuple-element.34), channel_id=1, source_target_pairs={{1,0},{2,1},{3,2},{5,4},{6,5},{7,6},{9,8},{10,9},{11,10},{13,12},{... | collective-permute-start | bytes 138248 | tf_op jit(solution)/shard_map/ppermute | solution.py:21
  23.1 6.7 %collective-permute-start.5 = (bf16[10,18,1,128]{3,2,1,0:T(2,128)(2,1)S(1)}, bf16[10,18,1,128]{3,2,1,0:T(2,128)(2,1)S(1)}, u32[]{:S(2)}, u32[]{:S(2)}) collective-permute-start(bf16[10,18,1,128]{3,2,1,0:T(2,128)(2,1)S(1)} %get-tuple-element.35), channel_id=1, source_target_pairs={{0,1},{1,2},{2,3},{4,5},{5,6},{6,7},{8,9},{9,10},{10,11},{12,13},{... | collective-permute-start | bytes 138248 | tf_op jit(solution)/shard_map/ppermute | solution.py:19
  42.3 1.0 copy-start.1
  60.2 83.5 %all-reduce.4.cloned.1.call-start = ((), (), s32[]{:S(2)}) async-start(), calls=%async_computation.2 | async-start | bytes 442368 | tf_op jit(solution)/shard_map/psum | solution.py:86
  144.8 45.7 %copy-start.22 = (bf16[8,16,16,128]{3,2,1,0:T(8,128)(2,1)S(1)}, bf16[8,16,16,128]{3,2,1,0:T(8,128)(2,1)}, u32[]{:S(2)}) copy-start(bf16[8,16,16,128]{3,2,1,0:T(8,128)(2,1)} %get-tuple-element.43) | copy-start | bytes 1572868
  190.1 1.0 copy-start.20
  190.4 1.1 copy-start.19
  191.5 1.1 copy-start.18
  191.8 1.1 copy-start.3
  192.9 1.0 copy-start.17
  193.2 1.1 copy-start.27
  194.2 1.1 copy-start.16
  194.6 1.1 copy-start.15
  195.6 1.1 copy-start.26
  196.0 1.1 copy-start.14
  197.0 1.1 copy-start.13
  197.4 1.1 copy-start.2
  198.3 1.1 copy-start.12
  198.7 1.1 copy-start.11
  199.7 1.1 copy-start.25
  200.1 1.1 copy-start.10
  201.1 1.1 copy-start.9
  201.5 1.1 copy-start.24
  202.4 1.1 copy-start.8
  202.9 1.1 copy-start.7
  203.8 1.1 copy-start.21
  204.3 1.1 copy-start.6
  205.2 1.1 copy-start.5
  205.6 1.1 copy-start.23
  206.6 1.1 copy-start.4
Sparse Core Ops, SparseCore 0:
  60.3 45.2 reduce-scatter.1
  108.5 35.0 all-reduce.3
where the time goes:
time: 217 us; the launch traced here: 216 us
  waiting for transfers between devices  59 us (27%)
  blocking collectives  58.9 us (27%)
  matrix products  35 us (16%)
  local copies, waits for them, and re-layouts  24.4 us (11%)
  starting transfers between devices  15.8 us (7%)
  between operations  15.2 us (7%)
  other arithmetic  7.2 us (3%)
    psum x1, waiting for transfers between devices, on_device(): column_sum = lax.psum(local_terms, 'gz')  32.5 us
    all_gather x1, blocking collectives, on_device(): lax.all_gather(std_float.astype(jnp.bfloat16), ('gx', 'gy'), axis=0, tile...  27.9 us
    dot_general x27, matrix products, filter_terms(): lax.dot_general(flat_in, view, (((0,), (0,)), ((), ())), preferred_elemen...  26.3 us
    reduce_scatter x1, waiting for transfers between devices, on_device(): lax.psum_scatter(column_sum, ('gx', 'gy'), scatter_dimension=0, tiled=True)  22.2 us
    psum x1, blocking collectives, on_device(): lax.psum((jnp.sum(raw_weight, axis=(0, 1)), jnp.sum(raw_weight * raw_weig...  16.7 us
    psum x1, blocking collectives, on_device(): lax.psum((local_grad, local_cross, local_square), ('gx', 'gy'))  14.4 us
    ppermute x3, starting transfers between devices, with_halo(): lax.ppermute(tail, axis, [(i, (i + 1) % count) for i in range(ends)])  11.8 us
    unnamed x61, local copies, waits for them, and re-layouts  9.64 us
  transfers between devices with their start and end apart: 8, of which 7 were waited for; matrix products, arithmetic and copies ran while one was open for 5% of the time, Pallas kernels for 0%

commit v1 on v0

--- a/solution.py
+++ b/solution.py
@@ -83,7 +83,7 @@
     std_whole = lax.all_gather(std_float.astype(jnp.bfloat16), ("gx", "gy"), axis=0, tiled=True)
     input_grad = input_rows(padded, extent, std_whole)
     local_terms = filter_terms(padded, flat_in, extent)
-    column_sum = lax.psum(local_terms, "gz")
+    column_sum = jnp.sum(lax.all_gather(local_terms, "gz"), axis=0)
     filter_grad = lax.psum_scatter(column_sum, ("gx", "gy"), scatter_dimension=0, tiled=True)
     local_grad = jnp.sum(filter_grad, axis=(0, 1))
     local_cross = jnp.sum(filter_grad * std_float, axis=(0, 1))

time: 217 us -> 323 us (1.49)
  waiting for transfers between devices: 59 us -> 152 us
  other arithmetic: 7.2 us -> 15.9 us
  local copies, waits for them, and re-layouts: 24.4 us -> 32 us
    all_gather x0 -> x1, waiting for transfers between devices: none -> 130 us  [on_device(): column_sum = jnp.sum(lax.all_gather(local_terms, 'gz'), axis=0)]
    psum x1 -> x0, waiting for transfers between devices: 32.5 us -> none  [on_device(): column_sum = lax.psum(local_terms, 'gz')]
    reduce_sum x0 -> x2, other arithmetic: none -> 9.72 us  [the longest x1 8.56 us: on_device(): column_sum = jnp.sum(lax.all_gather(local_terms, 'gz'), axis=0)]
    all_gather x0 -> x1, local copies, waits for them, and re-layouts: none -> 9.14 us  [on_device(): column_sum = jnp.sum(lax.all_gather(local_terms, 'gz'), axis=0)]
    reduce_scatter x1, waiting for transfers between devices: 22.2 us -> 15.1 us  [on_device(): lax.psum_scatter(column_sum, ('gx', 'gy'), scatter_dimension=0, tiled=True)]
    ppermute x3, waiting for transfers between devices: 1.4 us -> 5.15 us  [with_halo(): lax.ppermute(head, axis, [((i + 1) % count, i) for i in range(ends)])]
    unnamed x61 -> x63, local copies, waits for them, and re-layouts: 9.64 us -> 9.96 us
  transfers between devices with their start and end apart: 8 -> 8, of which waited for: 7 -> 7; matrix products, arithmetic and copies ran while one was open for 5% -> 3% of each run, Pallas kernels for 0% -> 0%
where the time goes in v1:
time: 323 us; the launch traced here: 322 us
  waiting for transfers between devices  152 us (47%)
  blocking collectives  56.5 us (17%)
  matrix products  34.8 us (11%)
  local copies, waits for them, and re-layouts  32 us (10%)
  other arithmetic  15.9 us (5%)
  starting transfers between devices  15.3 us (5%)
  between operations  15.2 us (5%)
    all_gather x1, waiting for transfers between devices, on_device(): column_sum = jnp.sum(lax.all_gather(local_terms, 'gz'), axis=0)  130 us
    all_gather x1, blocking collectives, on_device(): lax.all_gather(std_float.astype(jnp.bfloat16), ('gx', 'gy'), axis=0, tile...  28 us
    dot_general x27, matrix products, filter_terms(): lax.dot_general(flat_in, view, (((0,), (0,)), ((), ())), preferred_elemen...  26.1 us
    reduce_scatter x1, waiting for transfers between devices, on_device(): lax.psum_scatter(column_sum, ('gx', 'gy'), scatter_dimension=0, tiled=True)  15.1 us
    psum x1, blocking collectives, on_device(): lax.psum((jnp.sum(raw_weight, axis=(0, 1)), jnp.sum(raw_weight * raw_weig...  14.3 us
    psum x1, blocking collectives, on_device(): lax.psum((local_grad, local_cross, local_square), ('gx', 'gy'))  14.2 us
    ppermute x3, starting transfers between devices, with_halo(): lax.ppermute(tail, axis, [(i, (i + 1) % count) for i in range(ends)])  11.2 us
    unnamed x63, local copies, waits for them, and re-layouts  9.96 us
  transfers between devices with their start and end apart: 8, of which 7 were waited for; matrix products, arithmetic and copies ran while one was open for 3% of the time, Pallas kernels for 0%

profile of v1, /device:TPU:0, one launch (start us, length us, event | category | flops | bytes accessed | tf_op | source)
XLA Modules:
  0.0 321.7 jit_solution(10586339014623994114)
XLA Ops:
  7.2 0.9 fusion.68
  8.2 2.4 collective-permute-start
  10.6 1.3 collective-permute-start.1
  11.9 1.4 constant_dynamic-update-slice_fusion.5
  13.8 4.2 %collective-permute-start.2 = (bf16[10,1,16,128]{3,2,1,0:T(8,128)(2,1)S(1)}, bf16[10,1,16,128]{3,2,1,0:T(8,128)(2,1)S(1)}, u32[]{:S(2)}, u32[]{:S(2)}) collective-permute-start(bf16[10,1,16,128]{3,2,1,0:T(8,128)(2,1)S(1)} %get-tuple-element.44), channel_id=1, source_target_pairs={{0,4},{4,8},{8,12},{1,5},{5,9},{9,13},{2,6},{6,10},{10,14},{3,7},{... | collective-permute-start | bytes 122888 | tf_op jit(solution)/shard_map/ppermute | solution.py:19
  18.0 1.3 collective-permute-start.3
  19.7 4.2 %collective-permute-done.3 = bf16[10,1,16,128]{3,2,1,0:T(8,128)(2,1)S(1)} collective-permute-done((bf16[10,1,16,128]{3,2,1,0:T(8,128)(2,1)S(1)}, bf16[10,1,16,128]{3,2,1,0:T(8,128)(2,1)S(1)}, u32[]{:S(2)}, u32[]{:S(2)}) %collective-permute-start.3) | collective-permute-done | bytes 40992 | tf_op jit(solution)/shard_map/ppermute | solution.py:21
  24.0 1.3 collective-permute-start.4
  25.3 4.6 %collective-permute-start.5 = (bf16[10,18,1,128]{3,2,1,0:T(2,128)(2,1)S(1)}, bf16[10,18,1,128]{3,2,1,0:T(2,128)(2,1)S(1)}, u32[]{:S(2)}, u32[]{:S(2)}) collective-permute-start(bf16[10,18,1,128]{3,2,1,0:T(2,128)(2,1)S(1)} %get-tuple-element.34), channel_id=1, source_target_pairs={{0,1},{1,2},{2,3},{4,5},{5,6},{6,7},{8,9},{9,10},{10,11},{12,13},{... | collective-permute-start | bytes 138248 | tf_op jit(solution)/shard_map/ppermute | solution.py:19
  30.5 1.5 collective-permute-done.5
  32.0 0.8 pad_maximum_fusion.2
  32.9 1.0 fusion.29
  33.8 1.0 fusion.10
  34.8 1.0 fusion.28
  35.8 1.0 fusion.27
  36.7 1.0 fusion.9
  37.7 1.0 fusion.26
  38.7 1.0 fusion.25
  39.6 1.0 fusion.8
  40.6 1.0 fusion.24
  41.5 1.0 fusion.23
  42.5 1.0 fusion.7
  43.5 1.0 fusion.22
  44.5 1.0 fusion.21
  45.5 1.0 fusion.20
  46.5 1.0 fusion.19
  47.4 1.0 fusion.18
  48.4 1.0 fusion.6
  49.4 1.0 fusion.17
  50.3 1.0 fusion.16
  51.3 1.0 fusion.5
  52.3 1.0 fusion.15
  53.2 1.0 fusion.14
  54.2 1.0 fusion.4
  55.2 1.0 fusion.13
  56.2 1.0 fusion.12
  57.1 1.0 fusion.3
  58.1 1.0 fusion.11
  59.3 129.6 %all-gather.3.cloned.1.call-done = f32[512,27,128]{0,2,1:T(8,128)} async-done(((f32[128,27,128]{0,2,1:T(8,128)}), f32[512,27,128]{0,2,1:T(8,128)}) %all-gather.3.cloned.1.call-update) | async-done | bytes 7077904 | tf_op jit(solution)/shard_map/all_gather | solution.py:86
  188.9 9.1 %reshape.148 = f32[4,128,27,128]{1,0,3,2:T(4,128)} reshape(f32[512,27,128]{0,2,1:T(8,128)} %all-gather.3.cloned.1.call-done) | data formatting | bytes 14155776 | tf_op jit(solution)/shard_map/all_gather | solution.py:86
  198.1 8.6 %reduce_sum.65 = f32[128,27,128]{0,2,1:T(8,128)} reduce(f32[4,128,27,128]{1,0,3,2:T(4,128)} %reshape.148, f32[]{:T(128)} %constant.15.clone.1), dimensions={0}, to_apply=%region_4.0 | reduce | flops 1327104 | bytes 8847364 | tf_op jit(solution)/shard_map/reduce_sum | solution.py:86
  206.6 3.1 copy.14
  209.8 0.9 copy-done.28
  210.8 14.3 %all-reduce.1 = (f32[128]{0:T(128)S(1)}, f32[128]{0:T(128)S(1)}) all-reduce(f32[128]{0:T(128)S(1)} %get-tuple-element.7, f32[128]{0:T(128)S(1)} %get-tuple-element.6), channel_id=1, replica_groups=mesh['gx'=2,'gy'=4,'gz'=4] {'gx','gy'}, use_global_device_ids=true, to_apply=%region_1.0 | all-reduce | flops 256 | bytes 2048 | tf_op jit(solution)/shard_map/psum | solution.py:75
  225.1 1.9 slice.299
  227.0 1.9 slice.338
  228.8 1.7 fusion.32
  230.5 3.6 %fusion.65 = (bf16[8,16,16,128]{3,2,1,0:T(8,128)(2,1)S(1)}, bf16[8,16,16,128]{3,2,1,0:T(8,128)(2,1)}, bf16[8,16,16,128]{3,2,1,0:T(8,128)(2,1)}, bf16[8,16,16,128...) fusion(bf16[10,18,17,128]{3,2,1,0:T(8,128)(2,1)S(1)} %get-tuple, ...), kind=kLoop, calls=%fused_computation.177 | loop fusion | bytes 18874368 | tf_op jit(solution)/shard_map/slice | solution.py:29
  234.2 15.1 %reduce-scatter.2.cloned.1.call-done = f32[16,27,128]{2,1,0:T(8,128)} async-done(((f32[128,27,128]{2,1,0:T(8,128)}), f32[16,27,128]{2,1,0:T(8,128)}) %reduce-scatter.2.cloned.1.call-update) | async-done | bytes 221200 | tf_op jit(solution)/shard_map/reduce_scatter | solution.py:87
  249.2 1.0 multiply_reduce_fusion
  250.3 1.2 multiply_reduce_fusion.1
  251.4 14.2 %all-reduce = (f32[128]{0:T(128)S(1)}, f32[128]{0:T(128)S(1)}, f32[128]{0:T(128)S(1)}) all-reduce(f32[128]{0:T(128)S(1)} %multiply_reduce_fusion.1, f32[128]{0:T(128)S(1)} %get-tuple-element.5, f32[128]{0:T(128)S(1)} %get-tuple-element.4), channel_id=1, replica_groups=mesh['gx'=2,'gy'=4,'gz'=4] {'gx','gy'}, use_global_device_ids=true, to_apply=%region_9.0 | all-reduce | flops 384 | bytes 3072 | tf_op jit(solution)/shard_map/psum | solution.py:91
  267.0 1.9 multiply_multiply_fusion
  268.8 28.0 %all_gather.9 = bf16[128,27,128]{2,0,1:T(8,128)(2,1)S(1)} all-gather(bf16[16,27,128]{2,0,1:T(8,128)(2,1)S(1)} %get-tuple-element.52), channel_id=1, replica_groups=mesh['gx'=2,'gy'=4,'gz'=4] {'gx','gy'}, dimensions={0}, use_global_device_ids=true | all-gather | bytes 995328 | tf_op jit(solution)/shard_map/all_gather | solution.py:83
  298.6 0.7 copy-done.18
  299.9 0.7 copy-done.17
  301.3 0.7 copy-done.16
  302.7 0.7 copy-done.26
  304.1 0.6 copy-done.13
  305.5 0.6 copy-done.12
  306.9 0.6 copy-done.25
  308.2 0.6 copy-done.9
  309.6 0.6 copy-done.8
  313.8 1.1 fusion.2
  (93 shorter events, 13.3 us)
Async XLA Ops:
  7.2 25.7 %copy-start = (bf16[8,16,16,128]{3,2,1,0:T(8,128)(2,1)S(1)}, bf16[8,16,16,128]{3,2,1,0:T(8,128)(2,1)}, u32[]{:S(2)}) copy-start(bf16[8,16,16,128]{3,2,1,0:T(8,128)(2,1)} %param.4) | copy-start | bytes 1572868
  7.2 181.8 %all-gather.3.cloned.1.call-start = ((), (), s32[]{:S(2)}) async-start(), calls=%async_computation.2 | async-start | bytes 8847360 | tf_op jit(solution)/shard_map/all_gather | solution.py:86
  8.2 3.7 %collective-permute-start = (bf16[1,16,16,128]{3,2,1,0:T(8,128)(2,1)S(1)}, bf16[1,16,16,128]{3,2,1,0:T(8,128)(2,1)S(1)}, u32[]{:S(2)}, u32[]{:S(2)}) collective-permute-start(bf16[1,16,16,128]{3,2,1,0:T(8,128)(2,1)S(1)} %get-tuple-element.50), channel_id=1, source_target_pairs={{0,16},{1,17},{2,18},{3,19},{4,20},{5,21},{6,22},{7,23},{8,24},{9,... | collective-permute-start | bytes 196616 | tf_op jit(solution)/shard_map/ppermute | solution.py:19
  10.6 3.1 collective-permute-start.1
  13.3 40.9 %copy-start.30 = (bf16[9,16,16,128]{3,2,1,0:T(8,128)(2,1)}, bf16[9,16,16,128]{3,2,1,0:T(8,128)(2,1)S(1)}, u32[]{:S(2)}) copy-start(bf16[9,16,16,128]{3,2,1,0:T(8,128)(2,1)S(1)} %get-tuple-element.46) | copy-start | bytes 1769476
  13.7 23.0 %copy-start.29 = (bf16[9,16,16,128]{3,2,1,0:T(8,128)(2,1)}, bf16[9,16,16,128]{3,2,1,0:T(8,128)(2,1)S(1)}, u32[]{:S(2)}) copy-start(bf16[9,16,16,128]{3,2,1,0:T(8,128)(2,1)S(1)} %get-tuple-element.55) | copy-start | bytes 1769476
  13.8 5.9 %collective-permute-start.2 = (bf16[10,1,16,128]{3,2,1,0:T(8,128)(2,1)S(1)}, bf16[10,1,16,128]{3,2,1,0:T(8,128)(2,1)S(1)}, u32[]{:S(2)}, u32[]{:S(2)}) collective-permute-start(bf16[10,1,16,128]{3,2,1,0:T(8,128)(2,1)S(1)} %get-tuple-element.44), channel_id=1, source_target_pairs={{0,4},{4,8},{8,12},{1,5},{5,9},{9,13},{2,6},{6,10},{10,14},{3,7},{... | collective-permute-start | bytes 122888 | tf_op jit(solution)/shard_map/ppermute | solution.py:19
  18.0 5.9 %collective-permute-start.3 = (bf16[10,1,16,128]{3,2,1,0:T(8,128)(2,1)S(1)}, bf16[10,1,16,128]{3,2,1,0:T(8,128)(2,1)S(1)}, u32[]{:S(2)}, u32[]{:S(2)}) collective-permute-start(bf16[10,1,16,128]{3,2,1,0:T(8,128)(2,1)S(1)} %get-tuple-element.45), channel_id=1, source_target_pairs={{4,0},{8,4},{12,8},{5,1},{9,5},{13,9},{6,2},{10,6},{14,10},{7,3},{... | collective-permute-start | bytes 122888 | tf_op jit(solution)/shard_map/ppermute | solution.py:21
  24.0 6.4 %collective-permute-start.4 = (bf16[10,18,1,128]{3,2,1,0:T(2,128)(2,1)S(1)}, bf16[10,18,1,128]{3,2,1,0:T(2,128)(2,1)S(1)}, u32[]{:S(2)}, u32[]{:S(2)}) collective-permute-start(bf16[10,18,1,128]{3,2,1,0:T(2,128)(2,1)S(1)} %get-tuple-element.33), channel_id=1, source_target_pairs={{1,0},{2,1},{3,2},{5,4},{6,5},{7,6},{9,8},{10,9},{11,10},{13,12},{... | collective-permute-start | bytes 138248 | tf_op jit(solution)/shard_map/ppermute | solution.py:21
  25.3 6.7 %collective-permute-start.5 = (bf16[10,18,1,128]{3,2,1,0:T(2,128)(2,1)S(1)}, bf16[10,18,1,128]{3,2,1,0:T(2,128)(2,1)S(1)}, u32[]{:S(2)}, u32[]{:S(2)}) collective-permute-start(bf16[10,18,1,128]{3,2,1,0:T(2,128)(2,1)S(1)} %get-tuple-element.34), channel_id=1, source_target_pairs={{0,1},{1,2},{2,3},{4,5},{5,6},{6,7},{8,9},{9,10},{10,11},{12,13},{... | collective-permute-start | bytes 138248 | tf_op jit(solution)/shard_map/ppermute | solution.py:19
  44.5 1.0 copy-start.2
  59.1 190.1 %reduce-scatter.2.cloned.1.call-start = ((), (), s32[]{:S(2)}) async-start(), calls=%async_computation.1 | async-start | bytes 2359296 | tf_op jit(solution)/shard_map/reduce_scatter | solution.py:87
  209.8 0.9 copy-start.28
  234.1 62.7 %copy-start.22 = (bf16[8,16,16,128]{3,2,1,0:T(8,128)(2,1)S(1)}, bf16[8,16,16,128]{3,2,1,0:T(8,128)(2,1)}, u32[]{:S(2)}) copy-start(bf16[8,16,16,128]{3,2,1,0:T(8,128)(2,1)} %get-tuple-element.42) | copy-start | bytes 1572868
  296.9 1.0 copy-start.20
  297.2 1.1 copy-start.19
  298.2 1.1 copy-start.18
  298.5 1.1 copy-start.4
  299.6 1.0 copy-start.17
  299.9 1.1 copy-start.27
  301.0 1.1 copy-start.16
  301.3 1.1 copy-start.15
  302.3 1.1 copy-start.26
  302.7 1.1 copy-start.14
  303.7 1.1 copy-start.13
  304.1 1.1 copy-start.3
  305.0 1.1 copy-start.12
  305.5 1.1 copy-start.11
  306.4 1.1 copy-start.25
  306.8 1.1 copy-start.10
  307.8 1.1 copy-start.9
  308.2 1.1 copy-start.24
  309.2 1.1 copy-start.8
  309.6 1.1 copy-start.7
  310.5 1.1 copy-start.21
  311.0 1.1 copy-start.6
  311.9 1.1 copy-start.5
  312.4 1.1 copy-start.23
  313.3 1.6 copy-start.1
Sparse Core Ops, SparseCore 0:
  59.2 129.6 all-gather.2
  209.9 39.2 reduce-scatter.1
